TPU v7x, 32 devices: a whole 2x2x4 slice. The times are simulated.
32 devices in a mesh: aux: 4 (over z), orb: 8 (over y, x, core).
Axes of the slice: x: 2, y: 2, z: 4, core: 2. Of those that a mesh axis runs over, the one named last changes fastest.
Arguments:
- half: bfloat16 [64, 384, 3072], P('aux', 'orb'), may hold values from -1.25 to 1.25
- metric: bfloat16 [64, 64], P('aux'), may hold values from -1 to 2
- survive: int32 [4, 16, 24], P('aux', 'orb'), may hold values 0 or 1
Outputs:
- exchange_k: float32 [3072, 3072], P('orb', 'aux')
All inputs are finite; a program needn't handle non-finite values. No bound on the sum of `survive` on one device may be relied on, other than what follows from the above.
Results may differ from a plain program's by a relative error of at most 0.00098.
Values may be sent and summed in bfloat16 or wider, within the bound.
A program may use at most 128 MiB of HBM per device.

v0:
```python
import jax
import jax.numpy as jnp
from jax import lax
from jax.sharding import PartitionSpec as P


def shards(half, metric, survive):
    aux_local, occ_local, ao_count = half.shape
    blocks_aux, blocks_occ, blocks_ao = survive.shape
    gate = survive.astype(jnp.bfloat16)
    shaped = half.reshape(
        blocks_aux, aux_local, blocks_occ, occ_local // blocks_occ, blocks_ao, ao_count // blocks_ao
    )
    masked = (shaped * gate[:, None, :, None, :, None]).reshape(aux_local, occ_local, ao_count)
    portion = lax.all_gather(masked, "aux", axis=0, tiled=True)
    fit_total = jnp.dot(
        metric, portion.reshape(portion.shape[0], -1), preferred_element_type=jnp.float32
    )
    fitted = fit_total.astype(jnp.bfloat16).reshape(aux_local, occ_local, ao_count)
    group_width = ao_count // lax.axis_size("orb")
    row_start = lax.axis_index("orb") * group_width
    flat_rows = lax.all_gather(fitted, "orb", axis=1, tiled=True).reshape(-1, ao_count)
    left_rows = lax.dynamic_slice_in_dim(flat_rows, row_start, group_width, 1)
    partial_k = lax.dot_general(
        left_rows, flat_rows, (((0,), (0,)), ((), ())), preferred_element_type=jnp.float32
    )
    return lax.psum_scatter(partial_k, "aux", scatter_dimension=1, tiled=True)


def solution(mesh):
    return jax.shard_map(
        shards,
        mesh=mesh,
        in_specs=(P("aux", "orb", None), P("aux", None), P("aux", "orb", None)),
        out_specs=P("orb", "aux"),
        check_vma=False,
    )
```

profile of v0, /device:TPU:0, one launch (start us, length us, event | category | flops | bytes accessed | tf_op | source)
XLA Modules:
  0.0 656.1 jit_solution(17843219238067424248)
XLA Ops:
  6.5 0.0 copy-start
  6.5 0.0 all-gather.3.cloned.1.call-start
  6.5 0.7 convert_bitcast_fusion
  7.2 0.1 mul.21
  7.4 5.1 broadcast_multiply_fusion
  12.5 0.0 all-gather.3.cloned.1.call-update
  12.5 0.0 all-gather.5.cloned.1.call-start
  12.6 325.4 %all-gather.3.cloned.1.call-done = bf16[64,48,3072]{2,1,0:T(8,128)(2,1)} async-done(((bf16[16,48,3072]{2,1,0:T(8,128)(2,1)}), bf16[64,48,3072]{2,1,0:T(8,128)(2,1)}) %all-gather.3.cloned.1.call-update) | async-done | bytes 18874384 | tf_op jit(solution)/shard_map/all_gather | solution.py:15
  338.0 17.5 %copy.5 = bf16[8,8,48,3072]{3,1,2,0:T(8,128)(2,1)S(1)} copy(bf16[8,8,48,3072]{3,2,1,0:T(8,128)(2,1)} %bitcast.18) | data formatting | bytes 37748736
  355.5 0.0 copy-done
  355.5 2.7 convolution_convert_fusion
  358.3 4.7 copy.6
  363.0 0.0 all-gather.5.cloned.1.call-update
  363.0 0.0 reduce-scatter.2.cloned.1.call-start
  363.1 178.4 %all-gather.5.cloned.1.call-done = bf16[16,384,3072]{2,1,0:T(8,128)(2,1)} async-done(((bf16[16,48,3072]{2,1,0:T(8,128)(2,1)}), bf16[16,384,3072]{2,1,0:T(8,128)(2,1)}) %all-gather.5.cloned.1.call-update) | async-done | bytes 37748752 | tf_op jit(solution)/shard_map/all_gather | solution.py:22
  541.5 0.0 copy-start.1
  541.5 22.4 %fusion = f32[384,3072]{1,0:T(8,128)} fusion(bf16[6144,3072]{1,0:T(8,128)(2,1)} %bitcast.22, s32[]{:T(128)S(6)} %select_n.3), kind=kOutput, calls=%fused_computation.1 | convolution fusion | flops 14495514624 | bytes 47185924 | tf_op jit(solution)/shard_map/dot_general | solution.py:24
  563.9 0.0 reduce-scatter.2.cloned.1.call-update
  563.9 85.6 %reduce-scatter.2.cloned.1.call-done = f32[384,768]{1,0:T(8,128)} async-done(((f32[384,3072]{1,0:T(8,128)}), f32[384,768]{1,0:T(8,128)}) %reduce-scatter.2.cloned.1.call-update) | async-done | bytes 1179664 | tf_op jit(solution)/shard_map/reduce_scatter | solution.py:27
  649.5 0.0 copy-done.1
  (1 shorter events, 0.0 us)
Async XLA Ops:
  6.5 349.0 %copy-start = (bf16[16,64]{1,0:T(8,128)(2,1)S(1)}, bf16[16,64]{1,0:T(8,128)(2,1)}, u32[]{:S(2)}) copy-start(bf16[16,64]{1,0:T(8,128)(2,1)} %param.4) | copy-start | bytes 6148
  6.5 331.5 %all-gather.3.cloned.1.call-start = ((), (), s32[]{:S(2)}) async-start(), calls=%async_computation.1 | async-start | bytes 23592960 | tf_op jit(solution)/shard_map/all_gather | solution.py:15
  12.5 528.9 %all-gather.5.cloned.1.call-start = ((), (), s32[]{:S(2)}) async-start(), calls=%async_computation.2 | async-start | bytes 42467328 | tf_op jit(solution)/shard_map/all_gather | solution.py:22
  363.0 286.5 %reduce-scatter.2.cloned.1.call-start = ((), (), s32[]{:S(2)}) async-start(), calls=%async_computation.3 | async-start | bytes 5898240 | tf_op jit(solution)/shard_map/reduce_scatter | solution.py:27
  541.5 108.1 %copy-start.1 = (bf16[16,64]{1,0:T(8,128)(2,1)S(1)}, bf16[16,64]{1,0:T(8,128)(2,1)}, u32[]{:S(2)}) copy-start(bf16[16,64]{1,0:T(8,128)(2,1)} %param.4) | copy-start | bytes 6148
Sparse Core Ops, SparseCore 0:
  12.7 325.2 all-gather.2
  363.2 178.2 all-gather.4
  564.0 85.4 reduce-scatter.1
where the time goes:
time: 656 us
  waiting for transfers between devices  589 us (90%)
  matrix products  25.2 us (4%)
  local copies, waits for them, and re-layouts  22.4 us (3%)
  between operations  13.2 us (2%)
    all_gather x1, waiting for transfers between devices, shards(): portion = lax.all_gather(masked, 'aux', axis=0, tiled=True)  325 us
    all_gather x1, waiting for transfers between devices, shards(): lax.all_gather(fitted, 'orb', axis=1, tiled=True).reshape(-1, ao_count)  178 us
    reduce_scatter x1, waiting for transfers between devices, shards(): return lax.psum_scatter(partial_k, 'aux', scatter_dimension=1, tiled=True)  85.6 us
    dot_general x1, matrix products, shards(): lax.dot_general(left_rows, flat_rows, (((0,), (0,)), ((), ())), preferred...  22.4 us
    unnamed x7, local copies, waits for them, and re-layouts  22.3 us
  transfers between devices with their start and end apart: 3, of which 3 were waited for; matrix products, arithmetic and copies ran while one was open for 0% of the time, Pallas kernels for 0%

commit v1 on v0

--- a/solution.py
+++ b/solution.py
@@ -12,7 +12,14 @@
         blocks_aux, aux_local, blocks_occ, occ_local // blocks_occ, blocks_ao, ao_count // blocks_ao
     )
     masked = (shaped * gate[:, None, :, None, :, None]).reshape(aux_local, occ_local, ao_count)
-    portion = lax.all_gather(masked, "aux", axis=0, tiled=True)
+    devices = lax.axis_size("aux")
+    right = [(i, (i + 1) % devices) for i in range(devices)]
+    parts = [masked]
+    for far in range(1, devices):
+        parts = [lax.ppermute(parts[0], "aux", right), *parts]
+    whole = jnp.concatenate(parts, axis=0)
+    places = (lax.axis_index("aux") + 1) * parts[-1].shape[0]
+    portion = jnp.roll(whole, places, axis=0)
     fit_total = jnp.dot(
         metric, portion.reshape(portion.shape[0], -1), preferred_element_type=jnp.float32
     )

time: 656 us -> 709 us (1.081)
  local copies, waits for them, and re-layouts: 22.4 us -> 80.3 us
  waiting for transfers between devices: 589 us -> 576 us
    all_gather x1 -> x0, waiting for transfers between devices: 325 us -> none  [shards(): portion = lax.all_gather(masked, 'aux', axis=0, tiled=True)]
    ppermute x0 -> x3, waiting for transfers between devices: none -> 313 us  [shards(): parts = [lax.ppermute(parts[0], 'aux', right), *parts]]
    unnamed x7 -> x21, local copies, waits for them, and re-layouts: 22.3 us -> 70.7 us
    dynamic_slice x0 -> x1, local copies, waits for them, and re-layouts: none -> 9.46 us  [shards(): portion = jnp.roll(whole, places, axis=0)]
  transfers between devices with their start and end apart: 3 -> 5, of which waited for: 3 -> 5; matrix products, arithmetic and copies ran while one was open for 0% -> 0% of each run, Pallas kernels for 0% -> 0%
where the time goes in v1:
time: 709 us
  waiting for transfers between devices  576 us (81%)
  local copies, waits for them, and re-layouts  80.3 us (11%)
  matrix products  25.2 us (4%)
  between operations  13.5 us (2%)
  other arithmetic  10.7 us (2%)
    ppermute x3, waiting for transfers between devices, shards(): parts = [lax.ppermute(parts[0], 'aux', right), *parts]  313 us
    all_gather x1, waiting for transfers between devices, shards(): lax.all_gather(fitted, 'orb', axis=1, tiled=True).reshape(-1, ao_count)  177 us
    reduce_scatter x1, waiting for transfers between devices, shards(): return lax.psum_scatter(partial_k, 'aux', scatter_dimension=1, tiled=True)  85.6 us
    unnamed x21, local copies, waits for them, and re-layouts  70.7 us
    dot_general x1, matrix products, shards(): lax.dot_general(left_rows, flat_rows, (((0,), (0,)), ((), ())), preferred...  22.4 us
  transfers between devices with their start and end apart: 5, of which 5 were waited for; matrix products, arithmetic and copies ran while one was open for 0% of the time, Pallas kernels for 0%

profile of v1, /device:TPU:0, one launch (start us, length us, event | category | flops | bytes accessed | tf_op | source)
XLA Modules:
  0.0 708.7 jit_solution(3638923824115434351)
XLA Ops:
  6.5 0.0 copy-start
  6.5 0.0 all-gather.2.cloned.1.call-start
  6.5 0.7 convert_bitcast_fusion
  7.2 0.1 mul.24
  7.4 0.0 slice-start
  7.4 3.0 broadcast_multiply_fusion
  10.4 3.1 collective-permute-start
  13.5 103.8 %collective-permute-done = bf16[16,48,3072]{2,1,0:T(8,128)(2,1)S(1)} collective-permute-done((bf16[16,48,3072]{2,1,0:T(8,128)(2,1)S(1)}, bf16[16,48,3072]{2,1,0:T(8,128)(2,1)S(1)}, u32[]{:S(2)}, u32[]{:S(2)}) %collective-permute-start) | collective-permute-done | bytes 4718624 | tf_op jit(solution)/shard_map/ppermute | solution.py:19
  117.4 0.0 copy-start.1
  117.4 2.1 copy-done.1
  119.4 0.0 collective-permute-start.1
  119.4 104.9 %collective-permute-done.1 = bf16[16,48,3072]{2,1,0:T(8,128)(2,1)} collective-permute-done((bf16[16,48,3072]{2,1,0:T(8,128)(2,1)S(1)}, bf16[16,48,3072]{2,1,0:T(8,128)(2,1)}, u32[]{:S(2)}, u32[]{:S(2)}) %collective-permute-start.1) | collective-permute-done | bytes 4718624 | tf_op jit(solution)/shard_map/ppermute | solution.py:19
  224.3 0.0 collective-permute-start.2
  224.3 0.0 slice-start.2
  224.3 0.0 slice-start.1
  224.3 104.2 %collective-permute-done.2 = bf16[16,48,3072]{2,1,0:T(8,128)(2,1)} collective-permute-done((bf16[16,48,3072]{2,1,0:T(8,128)(2,1)}, bf16[16,48,3072]{2,1,0:T(8,128)(2,1)}, u32[]{:S(2)}, u32[]{:S(2)}) %collective-permute-start.2) | collective-permute-done | bytes 4718624 | tf_op jit(solution)/shard_map/ppermute | solution.py:19
  328.6 4.9 constant_dynamic-update-slice_fusion.7
  333.5 0.0 slice-start.3
  333.5 5.0 constant_dynamic-update-slice_fusion.6
  338.5 0.0 slice-done.2
  338.5 0.0 slice-done.3
  338.5 2.7 constant_dynamic-update-slice_fusion.5
  341.2 0.0 slice-done
  341.2 0.0 slice-done.1
  341.2 3.5 constant_dynamic-update-slice_fusion.4
  344.6 5.0 constant_dynamic-update-slice_fusion.3
  349.6 5.0 constant_dynamic-update-slice_fusion.2
  354.6 2.6 constant_dynamic-update-slice_fusion.1
  357.2 3.6 constant_dynamic-update-slice_fusion
  360.7 9.5 %constant_dynamic-slice_fusion = bf16[64,48,3072]{2,1,0:T(8,128)(2,1)S(1)} fusion(bf16[128,48,3072]{2,1,0:T(8,128)(2,1)} %constant_dynamic-update-slice_fusion, s32[]{:T(128)S(6)} %select_n.17), kind=kLoop, calls=%fused_computation.14 | loop fusion | bytes 37748740 | tf_op jit(solution)/shard_map/jit(_roll_dynamic)/dynamic_slice | solution.py:22
  370.2 38.7 %copy.5 = bf16[8,8,48,3072]{3,1,2,0:T(8,128)(2,1)S(1)} copy(bf16[8,8,48,3072]{3,2,1,0:T(8,128)(2,1)S(1)} %bitcast.17) | data formatting | bytes 37748736
  408.9 0.0 copy-done
  408.9 2.7 convolution_convert_fusion
  411.7 4.7 copy.6
  416.4 0.0 all-gather.2.cloned.1.call-update
  416.4 0.2 reduce-scatter.2.cloned.1.call-start
  416.6 177.1 %all-gather.2.cloned.1.call-done = bf16[16,384,3072]{2,1,0:T(8,128)(2,1)} async-done(((bf16[16,48,3072]{2,1,0:T(8,128)(2,1)}), bf16[16,384,3072]{2,1,0:T(8,128)(2,1)}) %all-gather.2.cloned.1.call-update) | async-done | bytes 37748752 | tf_op jit(solution)/shard_map/all_gather | solution.py:29
  593.8 22.4 %fusion = f32[384,3072]{1,0:T(8,128)} fusion(bf16[6144,3072]{1,0:T(8,128)(2,1)} %bitcast.28, s32[]{:T(128)S(6)} %select_n.18), kind=kOutput, calls=%fused_computation.1 | convolution fusion | flops 14495514624 | bytes 47185924 | tf_op jit(solution)/shard_map/dot_general | solution.py:31
  616.2 0.0 reduce-scatter.2.cloned.1.call-update
  616.2 85.6 %reduce-scatter.2.cloned.1.call-done = f32[384,768]{1,0:T(8,128)} async-done(((f32[384,3072]{1,0:T(8,128)}), f32[384,768]{1,0:T(8,128)}) %reduce-scatter.2.cloned.1.call-update) | async-done | bytes 1179664 | tf_op jit(solution)/shard_map/reduce_scatter | solution.py:34
  (3 shorter events, 0.0 us)
Async XLA Ops:
  6.5 402.4 %copy-start = (bf16[16,64]{1,0:T(8,128)(2,1)S(1)}, bf16[16,64]{1,0:T(8,128)(2,1)}, u32[]{:S(2)}) copy-start(bf16[16,64]{1,0:T(8,128)(2,1)} %param.4) | copy-start | bytes 6148
  6.5 587.2 %all-gather.2.cloned.1.call-start = ((), (), s32[]{:S(2)}) async-start(), calls=%async_computation.1 | async-start | bytes 42467328 | tf_op jit(solution)/shard_map/all_gather | solution.py:29
  7.4 333.8 %slice-start = ((s8[4718592]{0:T(1024)(128)(4,1)}), s8[524288]{0:T(1024)(128)(4,1)S(1)}, s32[]{:S(2)}) async-start(s8[4718592]{0:T(1024)(128)(4,1)} %bitcast.18), calls=%async_computation.3 | async-start | bytes 1048576
  10.4 106.9 %collective-permute-start = (bf16[16,48,3072]{2,1,0:T(8,128)(2,1)S(1)}, bf16[16,48,3072]{2,1,0:T(8,128)(2,1)S(1)}, u32[]{:S(2)}, u32[]{:S(2)}) collective-permute-start(bf16[16,48,3072]{2,1,0:T(8,128)(2,1)S(1)} %broadcast_multiply_fusion), channel_id=1, source_target_pairs={{0,8},{8,16},{16,24},{24,0},{1,9},{9,17},{17,25},{25,1},{2,10},{10... | collective-permute-start | bytes 14155784 | tf_op jit(solution)/shard_map/ppermute | solution.py:19
  117.4 2.1 copy-start.1
  119.4 104.9 %collective-permute-start.1 = (bf16[16,48,3072]{2,1,0:T(8,128)(2,1)S(1)}, bf16[16,48,3072]{2,1,0:T(8,128)(2,1)}, u32[]{:S(2)}, u32[]{:S(2)}) collective-permute-start(bf16[16,48,3072]{2,1,0:T(8,128)(2,1)S(1)} %collective-permute-done), channel_id=1, source_target_pairs={{0,8},{8,16},{16,24},{24,0},{1,9},{9,17},{17,25},{25,1},{2,10},{10... | collective-permute-start | bytes 14155784 | tf_op jit(solution)/shard_map/ppermute | solution.py:19
  224.3 104.2 %collective-permute-start.2 = (bf16[16,48,3072]{2,1,0:T(8,128)(2,1)}, bf16[16,48,3072]{2,1,0:T(8,128)(2,1)}, u32[]{:S(2)}, u32[]{:S(2)}) collective-permute-start(bf16[16,48,3072]{2,1,0:T(8,128)(2,1)} %collective-permute-done.1), channel_id=1, source_target_pairs={{0,8},{8,16},{16,24},{24,0},{1,9},{9,17},{17,25},{25,1},{2,10},{10... | collective-permute-start | bytes 14155784 | tf_op jit(solution)/shard_map/ppermute | solution.py:19
  224.3 114.2 %slice-start.2 = ((s8[4718592]{0:T(1024)(128)(4,1)}), s8[4194304]{0:T(1024)(128)(4,1)S(1)}, s32[]{:S(2)}) async-start(s8[4718592]{0:T(1024)(128)(4,1)} %bitcast.21), calls=%async_computation.5 | async-start | bytes 8388608
  224.3 116.8 %slice-start.1 = ((s8[4718592]{0:T(1024)(128)(4,1)}), s8[4194304]{0:T(1024)(128)(4,1)S(1)}, s32[]{:S(2)}) async-start(s8[4718592]{0:T(1024)(128)(4,1)} %bitcast.18), calls=%async_computation.4 | async-start | bytes 8388608
  333.5 5.0 slice-start.3
  416.4 285.4 %reduce-scatter.2.cloned.1.call-start = ((), (), s32[]{:S(2)}) async-start(), calls=%async_computation.2 | async-start | bytes 5898240 | tf_op jit(solution)/shard_map/reduce_scatter | solution.py:34
Sparse Core Ops, SparseCore 0:
  416.5 177.1 all-gather.1
  616.4 85.4 reduce-scatter.1
